TPU v7x, 512 devices: a whole 4x4x16 slice. The times are simulated.
512 devices in a mesh: segment: 16 (over z_hi, y, core), dp: 32 (over x, z_lo).
Axes of the slice: x: 4, y: 4, z: 16 (z_hi: 2, z_lo: 8; z = z_hi * 8 + z_lo), core: 2. Of those that a mesh axis runs over, the one named last changes fastest.
Arguments:
- token_ids: int32 [4096], P('dp'), may hold values from 0 to 152063, as said below
- table: bfloat16 [19008, 28672], P('segment', 'dp'), may hold values from -6 to 6
- out_grad: bfloat16 [4096, 3584], P('dp', 'segment'), may hold values from -6 to 6
Outputs:
- embedded: bfloat16 [4096, 3584], P('dp')
- table_grad: bfloat16 [19008, 28672], P('segment', 'dp')
Inputs may be any that keep to these rules, and one draw needn't show every extreme that they name: `token_ids`: in the 128 tokens of each data group, at most 16 ids lie in one segment's slice of 9504 rows with one residue modulo 8; in every data group some segment and residue has exactly 16.
All inputs are finite; a program needn't handle non-finite values.
Results may differ from a plain program's by a relative error of at most 0.001.
Values may be sent and summed in bfloat16 or wider, within the bound.
No kernel may reach another device: no remote copies, remote signals or barrier semaphores. Data moves between devices by JAX's collectives and lax.ppermute only.
A program may use at most 64 MiB of HBM per device.

v0:
```python
import itertools
import jax
import jax.numpy as jnp
from jax import lax
from jax.sharding import Mesh, PartitionSpec as P

D = 3584
PACK = 8
SLOTS = 16
NAMES = ("z_hi", "y", "core", "x", "z_lo")
SIZES = (2, 4, 2, 4, 8)
PLANE = ("y", "core", "x")
GROUPS = ("x", "z_lo")
QUARTERS = 4
WIDTH = D // QUARTERS
BF16 = jnp.bfloat16


def move(values, to):

    def flat(place):
        number = 0
        for size, at in zip(SIZES, place):
            number = number * size + at
        return number

    pairs = [
        (flat(place), flat(to(*place)))
        for place in itertools.product(*(range(size) for size in SIZES))
    ]
    return lax.ppermute(values, NAMES, pairs)


def lookup_code(z_hi, z_lo):
    return z_lo


def grad_code(z_hi, z_lo):
    return z_hi * 4 + z_lo // 4 * 2 + z_lo % 2


def grad_target(z_hi, y, core, x, z_lo):
    code = core * 4 + y ^ z_lo
    return (code // 4, y, core, x, code // 2 % 2 * 4 + 2 * z_hi + code % 2)


def groups_of_plane(code):
    at = jnp.arange(32, dtype=jnp.int32)
    y, core, x = (at // 8, at // 4 % 2, at % 4)
    return x * 8 + (core * 4 + y ^ code)


def pick_matrix(ids, section, z_hi, parity):
    segment = ids // section
    residue = ids % section % PACK
    bucket = segment * PACK + residue
    count = ids.shape[0]
    order = jnp.arange(count, dtype=jnp.int32)
    earlier = (bucket[:, None] == bucket[None, :]) & (order[None, :] < order[:, None])
    rank = jnp.sum(earlier.astype(jnp.int32), axis=1)
    here = (segment // 8 == z_hi) & (residue % 2 == parity)
    slot = jnp.where(here, (segment % 8 * 4 + residue // 2) * SLOTS + rank, -1)
    return (slot[:, None] == jnp.arange(32 * SLOTS, dtype=jnp.int32)[None, :]).astype(BF16)


def body(token_ids, table, out_grad):
    lines, width = table.shape
    section = lines * PACK
    tokens = token_ids.shape[0]
    z_hi, y, core, x, z_lo = (lax.axis_index(name) for name in NAMES)
    segment = (z_hi * 4 + y) * 2 + core
    residue = x * 2 + z_lo // 4
    parity = z_lo // 4
    place = core * 4 + y
    every_id = lax.all_to_all(
        jnp.broadcast_to(token_ids[None], (32, tokens)), GROUPS, 0, 0, tiled=True
    )
    code_f = lookup_code(z_hi, z_lo)
    code_b = grad_code(z_hi, z_lo)
    orders = jnp.concatenate([groups_of_plane(code_f), groups_of_plane(code_b)])
    ids = jnp.take(every_id, orders, axis=0)
    local = ids - segment * section
    owned = (local >= 0) & (local < section) & (local % PACK == residue)
    line = local // PACK
    steps = jnp.arange(tokens, dtype=jnp.int32)
    before = (steps[:, None] < steps[None, :]).astype(BF16)
    rank = jnp.dot(owned.astype(BF16), before, preferred_element_type=jnp.float32).astype(jnp.int32)
    slots = jnp.arange(SLOTS, dtype=jnp.int32)
    hit = owned[:, None, :] & (rank[:, None, :] == slots[None, :, None])
    row_of = jnp.sum(jnp.where(hit, line[:, None, :] + 1, 0), axis=2) - 1
    fetched = jnp.take(table, jnp.maximum(row_of[:32], 0).reshape(-1), axis=0)
    arrived = lax.all_to_all(fetched.reshape(32, SLOTS, width), PLANE, 0, 0, tiled=True)
    ids_f = lax.dynamic_index_in_dim(every_id, x * 8 + (place ^ code_f), 0, keepdims=False)
    pick_f = pick_matrix(ids_f, section, z_hi, parity)
    picked = jnp.dot(
        pick_f, arrived.reshape(32 * SLOTS, width), preferred_element_type=jnp.float32
    ).astype(BF16)

    def near(a, b, c, d, e):
        return (a, b, c, d, e ^ c * 4 + b)

    def far(a, b, c, d, e):
        return (1 - a, b, c, d, e ^ c * 4 + b)

    both = move(picked, near) + move(picked, far)
    quarter = both + lax.ppermute(both, "core", [(0, 1), (1, 0)])
    whole = lax.all_gather(quarter, "y")
    embedded = jnp.concatenate(
        [
            lax.dynamic_index_in_dim(whole, z_lo % 4 ^ part, 0, keepdims=False)
            for part in range(QUARTERS)
        ],
        axis=1,
    )
    halves = lax.all_gather(out_grad, ("y", "core"), axis=1, tiled=True)
    which = (place ^ z_lo) % 2
    piece = lax.dynamic_slice(halves, (0, which * width), (tokens, width))
    piece = move(piece, grad_target)
    ids_b = lax.dynamic_index_in_dim(every_id, x * 8 + (place ^ code_b), 0, keepdims=False)
    pick_b = pick_matrix(ids_b, section, z_hi, parity)
    packed = lax.dot_general(
        pick_b, piece, (((0,), (0,)), ((), ())), preferred_element_type=jnp.float32
    ).astype(BF16)
    returned = lax.all_to_all(packed.reshape(32, SLOTS, width), PLANE, 0, 0, tiled=True)
    target = row_of[32:].reshape(-1)
    spread = (jnp.arange(lines, dtype=jnp.int32)[:, None] == target[None, :]).astype(BF16)
    table_grad = jnp.dot(
        spread, returned.reshape(32 * SLOTS, width), preferred_element_type=jnp.float32
    ).astype(BF16)
    return (embedded, table_grad)


def solution(mesh):
    fine = Mesh(mesh.devices.reshape(SIZES), NAMES)
    segment, groups = (("z_hi", "y", "core"), ("x", "z_lo"))
    return jax.shard_map(
        body,
        mesh=fine,
        in_specs=(P(groups), P(segment, groups), P(groups, segment)),
        out_specs=(P(groups, None), P(segment, groups)),
        check_vma=False,
    )
```

profile of v0, /device:TPU:2, one launch (start us, length us, event | category | flops | bytes accessed | tf_op | source)
XLA Modules:
  0.0 144.1 jit_solution(15806224102012464601)
XLA Ops:
  0.6 0.0 copy-start
  0.6 1.4 broadcast_in_dim.37
  2.1 15.7 %all-to-all-start = ((s32[32,1,128]{2,1,0:T(1,128)}), s32[32,1,128]{2,1,0:T(1,128)S(1)}, u32[]{:S(2)}, u32[]{:S(2)}) async-start(s32[32,1,128]{2,1,0:T(1,128)} %broadcast_in_dim.37), calls=%async_computation | async-start | bytes 32768 | tf_op jit(solution)/shard_map/all_to_all | solution.py:75
  17.8 0.1 fusion.25
  17.9 0.1 compare_and_fusion
  18.0 11.0 %all-to-all-done = s32[32,1,128]{2,1,0:T(1,128)S(1)} async-done(((s32[32,1,128]{2,1,0:T(1,128)}), s32[32,1,128]{2,1,0:T(1,128)S(1)}, u32[]{:S(2)}, u32[]{:S(2)}) %all-to-all-start) | async-done | bytes 16416 | tf_op jit(solution)/shard_map/all_to_all | solution.py:75
  29.0 0.6 gather_fusion
  29.6 0.1 fusion.9
  29.7 0.1 fusion.11
  29.8 0.1 convolution_convert_fusion.3
  30.0 1.2 select_reduce_fusion
  31.2 0.1 reshape.480
  31.3 0.0 copy-done
  31.3 2.1 %gather_fusion.1 = bf16[512,896]{1,0:T(8,128)(2,1)S(1)} fusion(bf16[1188,896]{1,0:T(8,128)(2,1)S(1)} %copy-done, s32[1024]{0:T(1024)S(1)} %pad_clamp_fusion), kind=kCustom, calls=%fused_computation.1 | custom fusion | bytes 1837056 | tf_op jit(solution)/shard_map/jit(_take)/gather | solution.py:91
  33.3 1.1 broadcast_select_fusion
  34.4 6.7 %all-to-all-start.1 = ((bf16[32,16,896]{2,1,0:T(8,128)(2,1)}), bf16[32,16,896]{2,1,0:T(8,128)(2,1)S(1)}, u32[]{:S(2)}, u32[]{:S(2)}) async-start(bf16[32,16,896]{2,1,0:T(8,128)(2,1)} %broadcast_select_fusion), calls=%async_computation.1 | async-start | bytes 1835008 | tf_op jit(solution)/shard_map/all_to_all | solution.py:92
  41.2 21.6 %all_gather.11 = bf16[128,1792]{0,1:T(8,128)(2,1)S(1)} all-gather(bf16[128,224]{0,1:T(8,128)(2,1)} %param.5), channel_id=1, replica_groups=mesh['z_hi'=2,'y'=4,'core'=2,'x'=4,'z_lo'=8] {'y','core'}, dimensions={1}, use_global_device_ids=true | all-gather | bytes 516096 | tf_op jit(solution)/shard_map/all_gather | solution.py:115
  62.8 0.7 constant_dynamic-slice_fusion
  63.5 1.6 %collective-permute-start.3 = (bf16[128,896]{0,1:T(8,128)(2,1)}, bf16[128,896]{0,1:T(8,128)(2,1)S(1)}, u32[]{:S(2)}, u32[]{:S(2)}) collective-permute-start(bf16[128,896]{0,1:T(8,128)(2,1)} %constant_dynamic-slice_fusion), channel_id=1, source_target_pairs={{0,0},{1,1},{2,4},{3,5},{4,256},{5,257},{6,260},{7,261},{8,8},{9,9... | collective-permute-start | bytes 688136 | tf_op jit(solution)/shard_map/ppermute | solution.py:31
  65.1 0.2 convert_reduce_fusion
  65.3 0.0 collective-permute-done.3
  65.3 1.4 convolution_convert_fusion.1
  66.7 0.0 all-to-all-done.1
  66.7 23.3 %all-to-all-start.2 = ((bf16[32,16,896]{2,1,0:T(8,128)(2,1)}), bf16[32,16,896]{2,1,0:T(8,128)(2,1)}, u32[]{:S(2)}, u32[]{:S(2)}) async-start(bf16[32,16,896]{2,1,0:T(8,128)(2,1)} %bitcast.54), calls=%async_computation.2 | async-start | bytes 1835008 | tf_op jit(solution)/shard_map/all_to_all | solution.py:124
  90.0 0.2 convert_reduce_fusion.1
  90.2 0.4 convolution_convert_fusion.2
  90.6 9.8 %collective-permute-start.1 = (bf16[128,896]{1,0:T(8,128)(2,1)S(1)}, bf16[128,896]{1,0:T(8,128)(2,1)S(1)}, u32[]{:S(2)}, u32[]{:S(2)}) collective-permute-start(bf16[128,896]{1,0:T(8,128)(2,1)S(1)} %convolution_convert_fusion.2), channel_id=1, source_target_pairs={{0,256},{1,257},{2,258},{3,259},{4,260},{5,261},{6,262},{7,263},{8... | collective-permute-start | bytes 688136 | tf_op jit(solution)/shard_map/ppermute | solution.py:31
  100.4 0.7 collective-permute-start
  101.1 0.1 eq.165
  101.2 21.0 %collective-permute-done.1 = bf16[128,896]{1,0:T(8,128)(2,1)S(1)} collective-permute-done((bf16[128,896]{1,0:T(8,128)(2,1)S(1)}, bf16[128,896]{1,0:T(8,128)(2,1)S(1)}, u32[]{:S(2)}, u32[]{:S(2)}) %collective-permute-start.1) | collective-permute-done | bytes 229408 | tf_op jit(solution)/shard_map/ppermute | solution.py:31
  122.2 0.0 collective-permute-done
  122.2 0.1 add.524
  122.3 1.9 %collective-permute-start.2 = (bf16[128,896]{1,0:T(8,128)(2,1)S(1)}, bf16[128,896]{1,0:T(8,128)(2,1)S(1)}, u32[]{:S(2)}, u32[]{:S(2)}) collective-permute-start(bf16[128,896]{1,0:T(8,128)(2,1)S(1)} %add.524), channel_id=1, source_target_pairs={{0,32},{32,0},{1,33},{33,1},{2,34},{34,2},{3,35},{35,3},{4,36},{36... | collective-permute-start | bytes 688136 | tf_op jit(solution)/shard_map/ppermute | solution.py:106
  124.2 0.0 all-to-all-done.2
  124.2 3.9 %convolution_convert_fusion = bf16[1188,896]{1,0:T(8,128)(2,1)} fusion(bf16[512,896]{1,0:T(8,128)(2,1)} %bitcast.19, s32[512]{0:T(512)S(1)} %eq.165), kind=kOutput, calls=%fused_computation.2 | convolution fusion | flops 1091667456 | bytes 3048448 | tf_op jit(solution)/shard_map/dot_general | solution.py:127
  128.2 0.0 collective-permute-done.2
  128.2 0.1 add.525
  128.2 14.8 %all-gather = bf16[512,896]{1,0:T(8,128)(2,1)S(1)} all-gather(bf16[128,896]{1,0:T(8,128)(2,1)S(1)} %add.525), channel_id=2, replica_groups=mesh['z_hi'=2,'y'=4,'core'=2,'x'=4,'z_lo'=8] {'y'}, dimensions={0}, use_global_device_ids=true | all-gather | bytes 1146880 | tf_op jit(solution)/shard_map/all_gather | solution.py:107
  143.1 0.1 dynamic-slice_bitcast_fusion.3
  143.1 1.0 pad_maximum_fusion
  (11 shorter events, 0.1 us)
Async XLA Ops:
  0.6 30.6 %copy-start = (bf16[1188,896]{1,0:T(8,128)(2,1)S(1)}, bf16[1188,896]{1,0:T(8,128)(2,1)}, u32[]{:S(2)}) copy-start(bf16[1188,896]{1,0:T(8,128)(2,1)} %param.4) | copy-start | bytes 6386692
  2.1 26.9 %all-to-all-start = ((s32[32,1,128]{2,1,0:T(1,128)}), s32[32,1,128]{2,1,0:T(1,128)S(1)}, u32[]{:S(2)}, u32[]{:S(2)}) async-start(s32[32,1,128]{2,1,0:T(1,128)} %broadcast_in_dim.37), calls=%async_computation | async-start | bytes 32768 | tf_op jit(solution)/shard_map/all_to_all | solution.py:75
  34.4 32.3 %all-to-all-start.1 = ((bf16[32,16,896]{2,1,0:T(8,128)(2,1)}), bf16[32,16,896]{2,1,0:T(8,128)(2,1)S(1)}, u32[]{:S(2)}, u32[]{:S(2)}) async-start(bf16[32,16,896]{2,1,0:T(8,128)(2,1)} %broadcast_select_fusion), calls=%async_computation.1 | async-start | bytes 1835008 | tf_op jit(solution)/shard_map/all_to_all | solution.py:92
  63.5 1.8 %collective-permute-start.3 = (bf16[128,896]{0,1:T(8,128)(2,1)}, bf16[128,896]{0,1:T(8,128)(2,1)S(1)}, u32[]{:S(2)}, u32[]{:S(2)}) collective-permute-start(bf16[128,896]{0,1:T(8,128)(2,1)} %constant_dynamic-slice_fusion), channel_id=1, source_target_pairs={{0,0},{1,1},{2,4},{3,5},{4,256},{5,257},{6,260},{7,261},{8,8},{9,9... | collective-permute-start | bytes 688136 | tf_op jit(solution)/shard_map/ppermute | solution.py:31
  66.7 57.5 %all-to-all-start.2 = ((bf16[32,16,896]{2,1,0:T(8,128)(2,1)}), bf16[32,16,896]{2,1,0:T(8,128)(2,1)}, u32[]{:S(2)}, u32[]{:S(2)}) async-start(bf16[32,16,896]{2,1,0:T(8,128)(2,1)} %bitcast.54), calls=%async_computation.2 | async-start | bytes 1835008 | tf_op jit(solution)/shard_map/all_to_all | solution.py:124
  90.6 31.7 %collective-permute-start.1 = (bf16[128,896]{1,0:T(8,128)(2,1)S(1)}, bf16[128,896]{1,0:T(8,128)(2,1)S(1)}, u32[]{:S(2)}, u32[]{:S(2)}) collective-permute-start(bf16[128,896]{1,0:T(8,128)(2,1)S(1)} %convolution_convert_fusion.2), channel_id=1, source_target_pairs={{0,256},{1,257},{2,258},{3,259},{4,260},{5,261},{6,262},{7,263},{8... | collective-permute-start | bytes 688136 | tf_op jit(solution)/shard_map/ppermute | solution.py:31
  100.4 21.8 %collective-permute-start = (bf16[128,896]{1,0:T(8,128)(2,1)S(1)}, bf16[128,896]{1,0:T(8,128)(2,1)S(1)}, u32[]{:S(2)}, u32[]{:S(2)}) collective-permute-start(bf16[128,896]{1,0:T(8,128)(2,1)S(1)} %convolution_convert_fusion.2), channel_id=1, source_target_pairs={{0,0},{1,1},{2,2},{3,3},{4,4},{5,5},{6,6},{7,7},{8,8},{9,9},{10,10... | collective-permute-start | bytes 688136 | tf_op jit(solution)/shard_map/ppermute | solution.py:31
  122.3 5.9 %collective-permute-start.2 = (bf16[128,896]{1,0:T(8,128)(2,1)S(1)}, bf16[128,896]{1,0:T(8,128)(2,1)S(1)}, u32[]{:S(2)}, u32[]{:S(2)}) collective-permute-start(bf16[128,896]{1,0:T(8,128)(2,1)S(1)} %add.524), channel_id=1, source_target_pairs={{0,32},{32,0},{1,33},{33,1},{2,34},{34,2},{3,35},{35,3},{4,36},{36... | collective-permute-start | bytes 688136 | tf_op jit(solution)/shard_map/ppermute | solution.py:106
where the time goes:
time: 145 us; the launch traced here: 144 us
  starting transfers between devices  59.7 us (41%)
  blocking collectives  36.4 us (25%)
  waiting for transfers between devices  32.1 us (22%)
  matrix products  5.85 us (4%)
  local copies, waits for them, and re-layouts  5.02 us (3%)
  other arithmetic  4.18 us (3%)
    all_to_all x1, starting transfers between devices, body(): lax.all_to_all(packed.reshape(32, SLOTS, width), PLANE, 0, 0, tiled=True)  23.3 us
    all_gather x1, blocking collectives, body(): halves = lax.all_gather(out_grad, ('y', 'core'), axis=1, tiled=True)  21.6 us
    ppermute x3, waiting for transfers between devices, move(): return lax.ppermute(values, NAMES, pairs)  21.1 us
    all_to_all x1, starting transfers between devices, body(): lax.all_to_all(jnp.broadcast_to(token_ids[None], (32, tokens)), GROUPS, 0...  15.7 us
    all_gather x1, blocking collectives, body(): whole = lax.all_gather(quarter, 'y')  14.8 us
    ppermute x3, starting transfers between devices, move(): return lax.ppermute(values, NAMES, pairs)  12.1 us
    all_to_all x1, waiting for transfers between devices, body(): lax.all_to_all(jnp.broadcast_to(token_ids[None], (32, tokens)), GROUPS, 0...  11 us
    all_to_all x1, starting transfers between devices, body(): lax.all_to_all(fetched.reshape(32, SLOTS, width), PLANE, 0, 0, tiled=True)  6.71 us
  transfers between devices with their start and end apart: 7, of which 2 were waited for; matrix products, arithmetic and copies ran while one was open for 5% of the time, Pallas kernels for 0%

commit v1 on v0

--- a/solution.py
+++ b/solution.py
@@ -112,7 +112,10 @@
         ],
         axis=1,
     )
-    halves = lax.all_gather(out_grad, ("y", "core"), axis=1, tiled=True)
+    devices = lax.axis_size(("y", "core"))
+    pieces = jnp.stack([out_grad for _ in range(devices)])
+    pieces = lax.all_to_all(pieces, ("y", "core"), split_axis=0, concat_axis=0)
+    halves = jnp.concatenate(pieces, axis=1)
     which = (place ^ z_lo) % 2
     piece = lax.dynamic_slice(halves, (0, which * width), (tokens, width))
     piece = move(piece, grad_target)

time: 145 us -> 133 us (0.917)
  the two profiles are of different devices: /device:TPU:2 before, /device:TPU:4 now
where the time goes in v1:
time: 133 us; the launch traced here: 132 us
  starting transfers between devices  50.5 us (38%)
  waiting for transfers between devices  38.8 us (29%)
  blocking collectives  22.8 us (17%)
  local copies, waits for them, and re-layouts  7.28 us (5%)
  other arithmetic  7.1 us (5%)
  matrix products  4.67 us (4%)
    all_gather x1, blocking collectives, body(): whole = lax.all_gather(quarter, 'y')  22.8 us
    all_to_all x1, starting transfers between devices, body(): lax.all_to_all(jnp.broadcast_to(token_ids[None], (32, tokens)), GROUPS, 0...  15.7 us
    ppermute x3, waiting for transfers between devices, move(): return lax.ppermute(values, NAMES, pairs)  15.1 us
    all_to_all x1, waiting for transfers between devices, body(): lax.all_to_all(fetched.reshape(32, SLOTS, width), PLANE, 0, 0, tiled=True)  10.7 us
    ppermute x3, starting transfers between devices, move(): return lax.ppermute(values, NAMES, pairs)  10.5 us
    all_to_all x1, waiting for transfers between devices, body(): lax.all_to_all(jnp.broadcast_to(token_ids[None], (32, tokens)), GROUPS, 0...  10.1 us
    all_to_all x1, starting transfers between devices, body(): lax.all_to_all(packed.reshape(32, SLOTS, width), PLANE, 0, 0, tiled=True)  8.17 us
    all_to_all x1, starting transfers between devices, body(): lax.all_to_all(fetched.reshape(32, SLOTS, width), PLANE, 0, 0, tiled=True)  5.87 us
  transfers between devices with their start and end apart: 8, of which 4 were waited for; matrix products, arithmetic and copies ran while one was open for 10% of the time, Pallas kernels for 0%

profile of v1, /device:TPU:4, one launch (start us, length us, event | category | flops | bytes accessed | tf_op | source)
XLA Modules:
  0.0 132.1 jit_solution(4822787026784274148)
XLA Ops:
  0.6 0.0 copy-start
  0.6 1.4 %broadcast_in_dim.37 = s32[32,1,128]{2,1,0:T(1,128)} broadcast(s32[128]{0:T(128)} %param.3), dimensions={2} | broadcast | bytes 16896 | tf_op jit(solution)/shard_map/broadcast_in_dim | solution.py:76
  2.1 15.7 %all-to-all-start = ((s32[32,1,128]{2,1,0:T(1,128)}), s32[32,1,128]{2,1,0:T(1,128)S(1)}, u32[]{:S(2)}, u32[]{:S(2)}) async-start(s32[32,1,128]{2,1,0:T(1,128)} %broadcast_in_dim.37), calls=%async_computation | async-start | bytes 32768 | tf_op jit(solution)/shard_map/all_to_all | solution.py:75
  17.8 0.1 fusion.25
  17.9 0.1 compare_and_fusion
  18.0 10.1 %all-to-all-done = s32[32,1,128]{2,1,0:T(1,128)S(1)} async-done(((s32[32,1,128]{2,1,0:T(1,128)}), s32[32,1,128]{2,1,0:T(1,128)S(1)}, u32[]{:S(2)}, u32[]{:S(2)}) %all-to-all-start) | async-done | bytes 16416 | tf_op jit(solution)/shard_map/all_to_all | solution.py:75
  28.1 1.6 %stack.2 = bf16[8,128,224]{1,2,0:T(8,128)(2,1)} broadcast(bf16[128,224]{0,1:T(8,128)(2,1)} %param.5), dimensions={1,2} | broadcast | bytes 516096 | tf_op jit(solution)/shard_map/stack | solution.py:116
  29.7 4.5 %all-to-all-start.2 = ((bf16[8,128,224]{1,2,0:T(8,128)(2,1)}), bf16[8,128,224]{1,2,0:T(8,128)(2,1)S(1)}, u32[]{:S(2)}, u32[]{:S(2)}) async-start(bf16[8,128,224]{1,2,0:T(8,128)(2,1)} %stack.2), calls=%async_computation.2 | async-start | bytes 917504 | tf_op jit(solution)/shard_map/all_to_all | solution.py:117
  34.2 0.6 gather_fusion
  34.8 0.1 fusion.9
  34.9 0.1 fusion.11
  35.0 0.1 convolution_convert_fusion.3
  35.2 1.2 select_reduce_fusion
  36.3 0.0 copy-start.1
  36.3 0.6 copy-done.1
  37.0 0.1 reshape.488
  37.1 0.0 copy-done
  37.1 2.1 %gather_fusion.1 = bf16[512,896]{1,0:T(8,128)(2,1)S(1)} fusion(bf16[1188,896]{1,0:T(8,128)(2,1)S(1)} %copy-done, s32[1024]{0:T(1024)S(1)} %pad_clamp_fusion), kind=kCustom, calls=%fused_computation.1 | custom fusion | bytes 1837056 | tf_op jit(solution)/shard_map/jit(_take)/gather | solution.py:91
  39.1 0.7 broadcast_compare_fusion
  39.9 1.1 broadcast_select_fusion
  41.0 2.9 %all-to-all-done.2 = bf16[8,128,224]{1,2,0:T(8,128)(2,1)S(1)} async-done(((bf16[8,128,224]{1,2,0:T(8,128)(2,1)}), bf16[8,128,224]{1,2,0:T(8,128)(2,1)S(1)}, u32[]{:S(2)}, u32[]{:S(2)}) %all-to-all-start.2) | async-done | bytes 458784 | tf_op jit(solution)/shard_map/all_to_all | solution.py:117
  43.8 5.9 %all-to-all-start.1 = ((bf16[32,16,896]{2,1,0:T(8,128)(2,1)}), bf16[32,16,896]{2,1,0:T(8,128)(2,1)S(1)}, u32[]{:S(2)}, u32[]{:S(2)}) async-start(bf16[32,16,896]{2,1,0:T(8,128)(2,1)} %broadcast_select_fusion), calls=%async_computation.1 | async-start | bytes 1835008 | tf_op jit(solution)/shard_map/all_to_all | solution.py:92
  49.8 0.6 multiply_add_fusion
  50.4 0.2 convert_reduce_fusion.1
  50.6 0.7 constant_dynamic-slice_fusion
  51.3 1.6 %collective-permute-start.3 = (bf16[128,896]{0,1:T(8,128)(2,1)}, bf16[128,896]{0,1:T(8,128)(2,1)S(1)}, u32[]{:S(2)}, u32[]{:S(2)}) collective-permute-start(bf16[128,896]{0,1:T(8,128)(2,1)} %constant_dynamic-slice_fusion), channel_id=1, source_target_pairs={{0,0},{1,1},{2,4},{3,5},{4,256},{5,257},{6,260},{7,261},{8,8},{9,9... | collective-permute-start | bytes 688136 | tf_op jit(solution)/shard_map/ppermute | solution.py:31
  52.9 10.7 %all-to-all-done.1 = bf16[32,16,896]{2,1,0:T(8,128)(2,1)S(1)} async-done(((bf16[32,16,896]{2,1,0:T(8,128)(2,1)}), bf16[32,16,896]{2,1,0:T(8,128)(2,1)S(1)}, u32[]{:S(2)}, u32[]{:S(2)}) %all-to-all-start.1) | async-done | bytes 917536 | tf_op jit(solution)/shard_map/all_to_all | solution.py:92
  63.5 0.3 convolution_convert_fusion.2
  63.9 8.2 %collective-permute-start.1 = (bf16[128,896]{1,0:T(8,128)(2,1)S(1)}, bf16[128,896]{1,0:T(8,128)(2,1)S(1)}, u32[]{:S(2)}, u32[]{:S(2)}) collective-permute-start(bf16[128,896]{1,0:T(8,128)(2,1)S(1)} %convolution_convert_fusion.2), channel_id=1, source_target_pairs={{0,256},{1,257},{2,258},{3,259},{4,260},{5,261},{6,262},{7,263},{8... | collective-permute-start | bytes 688136 | tf_op jit(solution)/shard_map/ppermute | solution.py:31
  72.1 0.7 collective-permute-start
  72.8 0.9 convert_reduce_fusion
  73.7 0.1 eq.165
  73.8 15.1 %collective-permute-done.1 = bf16[128,896]{1,0:T(8,128)(2,1)S(1)} collective-permute-done((bf16[128,896]{1,0:T(8,128)(2,1)S(1)}, bf16[128,896]{1,0:T(8,128)(2,1)S(1)}, u32[]{:S(2)}, u32[]{:S(2)}) %collective-permute-start.1) | collective-permute-done | bytes 229408 | tf_op jit(solution)/shard_map/ppermute | solution.py:31
  88.9 0.0 collective-permute-done
  88.9 0.1 add.524
  89.0 5.9 %collective-permute-start.2 = (bf16[128,896]{1,0:T(8,128)(2,1)S(1)}, bf16[128,896]{1,0:T(8,128)(2,1)}, u32[]{:S(2)}, u32[]{:S(2)}) collective-permute-start(bf16[128,896]{1,0:T(8,128)(2,1)S(1)} %add.524), channel_id=1, source_target_pairs={{0,32},{32,0},{1,33},{33,1},{2,34},{34,2},{3,35},{35,3},{4,36},{36... | collective-permute-start | bytes 688136 | tf_op jit(solution)/shard_map/ppermute | solution.py:106
  94.8 0.0 collective-permute-done.3
  94.9 1.4 %convolution_convert_fusion.1 = bf16[512,896]{1,0:T(8,128)(2,1)} fusion(bf16[128,896]{0,1:T(8,128)(2,1)S(1)} %collective-permute-done.3, s32[128]{0:T(128)S(1)} %and_select_fusion.2), kind=kOutput, calls=%fused_computation.4 | convolution fusion | flops 118030336 | bytes 1147392 | tf_op jit(solution)/shard_map/dot_general | solution.py:124
  96.3 8.2 %all-to-all-start.3 = ((bf16[32,16,896]{2,1,0:T(8,128)(2,1)}), bf16[32,16,896]{2,1,0:T(8,128)(2,1)S(1)}, u32[]{:S(2)}, u32[]{:S(2)}) async-start(bf16[32,16,896]{2,1,0:T(8,128)(2,1)} %bitcast.20), calls=%async_computation.3 | async-start | bytes 1835008 | tf_op jit(solution)/shard_map/all_to_all | solution.py:127
  104.5 0.0 collective-permute-done.2
  104.5 1.0 add.525
  105.5 22.8 %all-gather = bf16[512,896]{1,0:T(8,128)(2,1)S(1)} all-gather(bf16[128,896]{1,0:T(8,128)(2,1)S(1)} %add.525), channel_id=2, replica_groups=mesh['z_hi'=2,'y'=4,'core'=2,'x'=4,'z_lo'=8] {'y'}, dimensions={0}, use_global_device_ids=true | all-gather | bytes 1146880 | tf_op jit(solution)/shard_map/all_gather | solution.py:107
  128.3 0.1 dynamic-slice_bitcast_fusion.3
  128.4 1.0 pad_maximum_fusion
  129.4 0.0 all-to-all-done.3
  129.4 2.8 %convolution_convert_fusion = bf16[1188,896]{1,0:T(8,128)(2,1)} fusion(bf16[512,896]{1,0:T(8,128)(2,1)S(1)} %bitcast.59, s32[512]{0:T(512)S(1)} %eq.165), kind=kOutput, calls=%fused_computation.2 | convolution fusion | flops 1091667456 | bytes 3048448 | tf_op jit(solution)/shard_map/dot_general | solution.py:130
  (9 shorter events, 0.1 us)
Async XLA Ops:
  0.6 36.4 %copy-start = (bf16[1188,896]{1,0:T(8,128)(2,1)S(1)}, bf16[1188,896]{1,0:T(8,128)(2,1)}, u32[]{:S(2)}) copy-start(bf16[1188,896]{1,0:T(8,128)(2,1)} %param.4) | copy-start | bytes 6386692
  2.1 26.0 %all-to-all-start = ((s32[32,1,128]{2,1,0:T(1,128)}), s32[32,1,128]{2,1,0:T(1,128)S(1)}, u32[]{:S(2)}, u32[]{:S(2)}) async-start(s32[32,1,128]{2,1,0:T(1,128)} %broadcast_in_dim.37), calls=%async_computation | async-start | bytes 32768 | tf_op jit(solution)/shard_map/all_to_all | solution.py:75
  29.7 14.1 %all-to-all-start.2 = ((bf16[8,128,224]{1,2,0:T(8,128)(2,1)}), bf16[8,128,224]{1,2,0:T(8,128)(2,1)S(1)}, u32[]{:S(2)}, u32[]{:S(2)}) async-start(bf16[8,128,224]{1,2,0:T(8,128)(2,1)} %stack.2), calls=%async_computation.2 | async-start | bytes 917504 | tf_op jit(solution)/shard_map/all_to_all | solution.py:117
  36.3 0.6 copy-start.1
  43.8 19.7 %all-to-all-start.1 = ((bf16[32,16,896]{2,1,0:T(8,128)(2,1)}), bf16[32,16,896]{2,1,0:T(8,128)(2,1)S(1)}, u32[]{:S(2)}, u32[]{:S(2)}) async-start(bf16[32,16,896]{2,1,0:T(8,128)(2,1)} %broadcast_select_fusion), calls=%async_computation.1 | async-start | bytes 1835008 | tf_op jit(solution)/shard_map/all_to_all | solution.py:92
  51.3 43.6 %collective-permute-start.3 = (bf16[128,896]{0,1:T(8,128)(2,1)}, bf16[128,896]{0,1:T(8,128)(2,1)S(1)}, u32[]{:S(2)}, u32[]{:S(2)}) collective-permute-start(bf16[128,896]{0,1:T(8,128)(2,1)} %constant_dynamic-slice_fusion), channel_id=1, source_target_pairs={{0,0},{1,1},{2,4},{3,5},{4,256},{5,257},{6,260},{7,261},{8,8},{9,9... | collective-permute-start | bytes 688136 | tf_op jit(solution)/shard_map/ppermute | solution.py:31
  63.9 25.0 %collective-permute-start.1 = (bf16[128,896]{1,0:T(8,128)(2,1)S(1)}, bf16[128,896]{1,0:T(8,128)(2,1)S(1)}, u32[]{:S(2)}, u32[]{:S(2)}) collective-permute-start(bf16[128,896]{1,0:T(8,128)(2,1)S(1)} %convolution_convert_fusion.2), channel_id=1, source_target_pairs={{0,256},{1,257},{2,258},{3,259},{4,260},{5,261},{6,262},{7,263},{8... | collective-permute-start | bytes 688136 | tf_op jit(solution)/shard_map/ppermute | solution.py:31
  72.1 16.8 %collective-permute-start = (bf16[128,896]{1,0:T(8,128)(2,1)S(1)}, bf16[128,896]{1,0:T(8,128)(2,1)S(1)}, u32[]{:S(2)}, u32[]{:S(2)}) collective-permute-start(bf16[128,896]{1,0:T(8,128)(2,1)S(1)} %convolution_convert_fusion.2), channel_id=1, source_target_pairs={{0,0},{1,1},{2,2},{3,3},{4,4},{5,5},{6,6},{7,7},{8,8},{9,9},{10,10... | collective-permute-start | bytes 688136 | tf_op jit(solution)/shard_map/ppermute | solution.py:31
  89.0 15.5 %collective-permute-start.2 = (bf16[128,896]{1,0:T(8,128)(2,1)S(1)}, bf16[128,896]{1,0:T(8,128)(2,1)}, u32[]{:S(2)}, u32[]{:S(2)}) collective-permute-start(bf16[128,896]{1,0:T(8,128)(2,1)S(1)} %add.524), channel_id=1, source_target_pairs={{0,32},{32,0},{1,33},{33,1},{2,34},{34,2},{3,35},{35,3},{4,36},{36... | collective-permute-start | bytes 688136 | tf_op jit(solution)/shard_map/ppermute | solution.py:106
  96.3 33.1 %all-to-all-start.3 = ((bf16[32,16,896]{2,1,0:T(8,128)(2,1)}), bf16[32,16,896]{2,1,0:T(8,128)(2,1)S(1)}, u32[]{:S(2)}, u32[]{:S(2)}) async-start(bf16[32,16,896]{2,1,0:T(8,128)(2,1)} %bitcast.20), calls=%async_computation.3 | async-start | bytes 1835008 | tf_op jit(solution)/shard_map/all_to_all | solution.py:127
